TPU v7x, 128 devices: a whole 4x4x4 slice. The times are simulated.
128 devices in a mesh: obs: 4 (over z), face: 32 (over x, y, core).
Axes of the slice: x: 4, y: 4, z: 4, core: 2. Of those that a mesh axis runs over, the one named last changes fastest.
Arguments:
- density: float32 [34, 32768], P(None, ('obs', 'face')), may hold values from 0.6 to 1.4
- velocity: float32 [3, 34, 32768], P(None, None, ('obs', 'face')), may hold values from -6 to 6
- pressure: float32 [34, 32768], P(None, ('obs', 'face')), may hold values from -6 to 6
- normal: float32 [3, 32768], P(None, ('obs', 'face')), may hold values from -1 to 1, as said below
- direction: float32 [128, 32, 3], P(('obs', 'face')), may hold values from -1 to 1, as said below
- weights: bfloat16 [128, 32, 768, 256], P(('obs', 'face')), may hold values from -0.21875 to 0.21875
- bin_index: int32 [128, 32], P(('obs', 'face')), may hold values from 0 to 31, as said below
- group_index: int32 [128, 32], P(('obs', 'face')), may hold values from 0 to 3
- item_count: int32 [128], P(('obs', 'face')), may hold values from 16 to 32, as said below
Outputs:
- signal: float32 [1024, 1024], P('face', 'obs')
Inputs may be any that keep to these rules, and one draw needn't show every extreme that they name: `bin_index`: no time block is named more than 2 times in one device's list; in every draw some device names a block 2 times among its live entries. `item_count`: some device has all 32 entries live. Each face's normal has unit length. Each entry's direction has unit length.
All inputs are finite; a program needn't handle non-finite values.
Results may differ from a plain program's by a relative error of at most 0.0029.
Values sent between devices are 32-bit elements; how exact they have to be, the bound alone decides.
A program may use at most 64 MiB of HBM per device.

v0:
```python
import jax
import jax.numpy as jnp
from jax import lax
from jax.sharding import PartitionSpec as P

SLOT_CAP = 2


def in_blocks(array, dim, count):
    before, after = (array.shape[:dim], array.shape[dim + 1 :])
    return jnp.moveaxis(array.reshape(*before, count, -1, *after), dim, 0)


def sum_at_owner(array, axis, dim):
    parts = in_blocks(array, dim, lax.axis_size(axis))
    arrived = lax.all_to_all(parts, axis, split_axis=0, concat_axis=0, tiled=True)
    return arrived.sum(axis=0)


def face_terms(dens, veloc, press, norms):
    normal_speed = veloc[0] * norms[0][None] + veloc[1] * norms[1][None] + veloc[2] * norms[2][None]
    flux = dens * normal_speed
    load_first = press * norms[0][None] + dens * veloc[0] * normal_speed
    load_second = press * norms[1][None] + dens * veloc[1] * normal_speed
    load_third = press * norms[2][None] + dens * veloc[2] * normal_speed
    thick = 0.5 * (flux[2:] - flux[:-2])
    return (thick, load_first, load_second, load_third)


def item_source(thick, load_first, load_second, load_third, heading):
    radial = heading[0] * load_first + heading[1] * load_second + heading[2] * load_third
    rate = 0.5 * (radial[2:] - radial[:-2])
    return jnp.concatenate([thick, rate, radial[1:-1]], axis=1).astype(jnp.bfloat16)


def local(
    density, velocity, pressure, normal, direction, weights, bin_index, group_index, item_count
):
    thick, load_first, load_second, load_third = face_terms(density, velocity, pressure, normal)
    headings = direction[0]
    matrices = weights[0]
    blocks_of = bin_index[0]
    groups_of = group_index[0]
    live_count = item_count[0]
    list_total = matrices.shape[0]
    steps = thick.shape[0]
    width = matrices.shape[2]
    n_face = lax.axis_size("face")
    n_obs = lax.axis_size("obs")

    def item_block(listed):
        heading = lax.dynamic_index_in_dim(headings, listed, 0, False)
        source = item_source(thick, load_first, load_second, load_third, heading)
        matrix = lax.dynamic_index_in_dim(matrices, listed, 0, False)
        return jnp.dot(source, matrix, preferred_element_type=jnp.float32)

    order = jnp.arange(list_total, dtype=jnp.int32)
    is_live = order < live_count
    matches = (
        (blocks_of[:, None] == blocks_of[None, :])
        & (order[:, None] > order[None, :])
        & is_live[None, :]
    )
    slot_index = blocks_of * SLOT_CAP + jnp.sum(matches.astype(jnp.int32), axis=1)

    def add_routed(listed, carried):
        outgoing, labels = carried
        target = slot_index[listed]
        outgoing = lax.dynamic_update_index_in_dim(outgoing, item_block(listed)[None], target, 0)
        labels = labels.at[target].set(groups_of[listed].astype(jnp.float32))
        return (outgoing, labels)

    empty_blocks = jnp.zeros((n_face * SLOT_CAP, steps, width), jnp.float32)
    empty_labels = jnp.zeros((n_face * SLOT_CAP,), jnp.float32)
    outgoing, labels = lax.fori_loop(0, live_count, add_routed, (empty_blocks, empty_labels))
    arrived, arrived_labels = (
        lax.all_to_all(
            outgoing.reshape(n_face, SLOT_CAP, steps, width),
            "face",
            split_axis=0,
            concat_axis=0,
            tiled=True,
        ),
        lax.all_to_all(
            labels.reshape(n_face, SLOT_CAP), "face", split_axis=0, concat_axis=0, tiled=True
        ),
    )
    selector = (
        arrived_labels.reshape(1, -1) == jnp.arange(n_obs, dtype=jnp.float32)[:, None]
    ).astype(jnp.float32)
    grouped = jnp.dot(
        selector,
        arrived.reshape(n_face * SLOT_CAP, steps * width),
        precision=lax.Precision.HIGHEST,
        preferred_element_type=jnp.float32,
    )
    owned = sum_at_owner(grouped.reshape(n_obs, steps, width), "obs", 0)
    return owned.reshape(steps, width)


def solution(mesh):
    placed = (
        P(None, ("obs", "face")),
        P(None, None, ("obs", "face")),
        P(None, ("obs", "face")),
        P(None, ("obs", "face")),
        P(("obs", "face"), None, None),
        P(("obs", "face"), None, None, None),
        P(("obs", "face"), None),
        P(("obs", "face"), None),
        P(("obs", "face")),
    )
    return jax.shard_map(
        local, mesh=mesh, in_specs=placed, out_specs=P("face", "obs"), check_vma=False
    )
```

profile of v0, /device:TPU:1, one launch (start us, length us, event | category | flops | bytes accessed | tf_op | source)
XLA Modules:
  0.0 285.3 jit_solution(10141828849065942715)
XLA Ops:
  5.8 212.3 %while.14 = (s32[]{:T(128)}, f32[64,32,256]{2,1,0:T(8,128)S(1)}, f32[64]{0:T(128)S(1)}, s32[]{:T(128)}, bf16[32,256]{1,0:T(8,128)(2,1)S(1)}, /*index=5*/f32[32,3...) while((s32[]{:T(128)}, f32[64,32,256]{2,1,0:T(8,128)S(1)}, ...), condition=%wide.wide.region_2.3_spmd, body=%wide.wide.region_1.2_spmd.sunk | while | flops 12798477 | bytes 729951 | solution.py:75
  7.1 1.8 multiply_add_fusion.3
  13.9 1.8 multiply_add_fusion.3
  20.7 1.8 multiply_add_fusion.3
  27.6 1.8 multiply_add_fusion.3
  34.4 1.8 multiply_add_fusion.3
  41.2 1.8 multiply_add_fusion.3
  48.1 1.8 multiply_add_fusion.3
  54.9 1.8 multiply_add_fusion.3
  61.7 1.8 multiply_add_fusion.3
  68.5 1.8 multiply_add_fusion.3
  75.4 1.8 multiply_add_fusion.3
  82.2 1.8 multiply_add_fusion.3
  89.0 1.8 multiply_add_fusion.3
  95.9 1.8 multiply_add_fusion.3
  130.0 1.8 multiply_add_fusion.3
  136.8 1.8 multiply_add_fusion.3
  143.7 1.8 multiply_add_fusion.3
  150.5 1.8 multiply_add_fusion.3
  218.2 22.0 %all_to_all.19 = f32[32,1,2]{2,1,0:T(1,128)S(1)} all-to-all(f32[32,1,2]{2,1,0:T(1,128)S(1)} %bitcast.95), channel_id=1, replica_groups=mesh['obs'=4,'face'=32] {'face'}, dimensions={0} | all-to-all | bytes 512 | tf_op jit(solution)/shard_map/all_to_all | solution.py:84
  240.2 4.3 %all-to-all-start.1 = ((f32[32,2,32,256]{3,2,1,0:T(8,128)}), f32[32,2,32,256]{3,2,1,0:T(8,128)S(1)}, u32[]{:S(2)}, u32[]{:S(2)}) async-start(f32[32,2,32,256]{3,2,1,0:T(8,128)} %bitcast.92), calls=%async_computation.1 | async-start | bytes 4194304 | tf_op jit(solution)/shard_map/all_to_all | solution.py:77
  245.8 27.1 %all-to-all-done.1 = f32[32,2,32,256]{3,2,1,0:T(8,128)S(1)} async-done(((f32[32,2,32,256]{3,2,1,0:T(8,128)}), f32[32,2,32,256]{3,2,1,0:T(8,128)S(1)}, u32[]{:S(2)}, u32[]{:S(2)}) %all-to-all-start.1) | async-done | bytes 2097184 | tf_op jit(solution)/shard_map/all_to_all | solution.py:77
  273.0 2.0 fusion.15
  275.0 9.7 %all_to_all.20 = f32[4,1,32,256]{3,2,1,0:T(8,128)S(1)} all-to-all(f32[4,1,32,256]{3,2,1,0:T(8,128)S(1)} %copy.16), channel_id=1, replica_groups=mesh['obs'=4,'face'=32] {'obs'}, dimensions={0} | all-to-all | bytes 262144 | tf_op jit(solution)/shard_map/all_to_all | solution.py:16
  (250 shorter events, 111.4 us)
Async XLA Ops:
  0.0 5.8 %copy-start.1 = (s32[1,32]{1,0:T(1,128)S(1)}, s32[1,32]{1,0:T(1,128)}, u32[]{:S(2)}) copy-start(s32[1,32]{1,0:T(1,128)} %param.20) | copy-start | bytes 388
  218.1 22.1 %copy-start = (f32[64,32,256]{2,1,0:T(8,128)}, f32[64,32,256]{2,1,0:T(8,128)S(1)}, u32[]{:S(2)}) copy-start(f32[64,32,256]{2,1,0:T(8,128)S(1)} %get-tuple-element.82) | copy-start | bytes 6291460
  240.2 32.8 %all-to-all-start.1 = ((f32[32,2,32,256]{3,2,1,0:T(8,128)}), f32[32,2,32,256]{3,2,1,0:T(8,128)S(1)}, u32[]{:S(2)}, u32[]{:S(2)}) async-start(f32[32,2,32,256]{3,2,1,0:T(8,128)} %bitcast.92), calls=%async_computation.1 | async-start | bytes 4194304 | tf_op jit(solution)/shard_map/all_to_all | solution.py:77
where the time goes:
time: 289 us; the launch traced here: 285 us
  loops' own time  75 us (26%)
  other arithmetic  67.4 us (23%)
  local copies, waits for them, and re-layouts  41.2 us (14%)
  matrix products  37.8 us (13%)
  blocking collectives  31.7 us (11%)
  waiting for transfers between devices  27.1 us (9%)
  starting transfers between devices  4.32 us (1%)
    another operation x1, loops' own time, local(): lax.fori_loop(0, live_count, add_routed, (empty_blocks, empty_labels))  75 us
    add x31, other arithmetic, item_source(): heading[0] * load_first + heading[1] * load_second + heading[2] * load_third  56.8 us
    dot_general x31, matrix products, item_block(): return jnp.dot(source, matrix, preferred_element_type=jnp.float32)  35.8 us
    all_to_all x1, waiting for transfers between devices, local(): lax.all_to_all(outgoing.reshape(n_face, SLOT_CAP, steps, width), 'face',...  27.1 us
    all_to_all x1, blocking collectives, local(): lax.all_to_all(labels.reshape(n_face, SLOT_CAP), 'face', split_axis=0, co...  22 us
    slice x31, local copies, waits for them, and re-layouts, item_source(): heading[0] * load_first + heading[1] * load_second + heading[2] * load_third  18.2 us
    dynamic_slice x31, local copies, waits for them, and re-layouts, add_routed(): target = slot_index[listed]  18 us
    all_to_all x1, blocking collectives, sum_at_owner(): lax.all_to_all(parts, axis, split_axis=0, concat_axis=0, tiled=True)  9.67 us
  transfers between devices with their start and end apart: 1, of which 1 were waited for; matrix products, arithmetic and copies ran while one was open for 0% of the time, Pallas kernels for 0%

commit v1 on v0

v1 whole, which is shorter than its diff:
```python
import functools

import jax
import jax.numpy as jnp
from jax import lax
from jax.experimental import pallas as pl
from jax.experimental.pallas import tpu as pltpu
from jax.sharding import PartitionSpec as P

ITEMS = 32
STEPS = 32
FACES = 256
HALF = 128
CHUNK = 4
CHUNKS = ITEMS // CHUNK
EMPTY = ITEMS

X, Y, Z = 0, 1, 2
PATHS = (
    (X, Z, Y),
    (Y, Z, X),
    (Z, X, Y),
    (X, Z, Y),
    (X, Z, Y),
    (Y, Z, X),
    (Z, Y, X),
    (Y, Z, X),
)
ORDER = (
    (1, 1), (2, 1), (0, 1), (5, 1), (6, 1), (3, 1),
    (1, 2), (2, 2), (0, 2), (4, 1), (7, 1), (3, 2), (6, 2), (5, 2),
    (1, 3), (2, 3), (0, 3), (4, 2), (7, 2), (3, 3), (6, 3), (5, 3),
    (1, 4), (2, 4), (0, 4), (4, 3), (7, 3), (3, 4), (6, 4), (5, 4),
    (4, 4), (7, 4),
)


def kernel(
    dens_hbm, veloc_hbm, press_hbm, norm_hbm, head_hbm, weight_hbm, bin_hbm, group_hbm, count_hbm,
    out_ref,
    dens, veloc, press, norms, head, bins, groups, count,
    faces, terms, thick, sources, matrices, own_first, own_second, other_first, other_second, table, table_there, look, look_there,
    acc, first_in, second_in, third_in,
    input_sem, matrix_sem, look_sem, send_sem, recv_sem,
):
    obs = lax.axis_index("obs")
    face = lax.axis_index("face")
    core = lax.rem(face, 2)
    chip = face // 2
    here = (chip // 4, lax.rem(chip, 4), obs)

    def at(axis, step):
        place = list(here)
        place[axis] = lax.rem(here[axis] + step, 4)
        return (place[2], (place[0] * 4 + place[1]) * 2 + core)

    partner = (obs, chip * 2 + (1 - core))
    own, other = (own_first, own_second), (other_first, other_second)

    inputs = [
        pltpu.make_async_copy(source, target, input_sem.at[place])
        for place, (source, target) in enumerate(
            (
                (bin_hbm, bins),
                (group_hbm, groups),
                (count_hbm, count),
                (head_hbm, head),
                (dens_hbm, dens),
                (veloc_hbm, veloc),
                (press_hbm, press),
                (norm_hbm, norms),
            )
        )
    ]
    for copy in inputs:
        copy.start()

    def matrix_copy(half, chunk):
        return pltpu.make_async_copy(
            weight_hbm.at[pl.ds(chunk * CHUNK, CHUNK), :, pl.ds(half * HALF, HALF)],
            matrices.at[half, pl.ds(chunk * CHUNK, CHUNK)],
            matrix_sem.at[half * CHUNKS + chunk],
        )

    for half in range(2):
        for chunk in range(CHUNKS):
            matrix_copy(half, chunk).start()

    barrier = pltpu.get_barrier_semaphore()
    greeted = [partner] + [at(axis, step) for axis in range(3) for step in (1, 2, 3)]
    for device in greeted:
        pl.semaphore_signal(
            barrier, inc=1, device_id=device, device_id_type=pl.DeviceIdType.MESH
        )

    sent = []

    def send(source, target, device):
        place = len(sent)
        copy = pltpu.make_async_remote_copy(
            src_ref=source,
            dst_ref=target,
            send_sem=send_sem.at[place],
            recv_sem=recv_sem.at[place],
            device_id=device,
            device_id_type=pl.DeviceIdType.MESH,
        )
        copy.start()
        sent.append(copy)
        return copy

    for half in range(2):
        own[half][EMPTY] = jnp.zeros((STEPS, HALF), jnp.float32)
        other[half][EMPTY] = jnp.zeros((STEPS, HALF), jnp.float32)

    for copy in inputs[:3]:
        copy.wait()
    rows = lax.broadcasted_iota(jnp.int32, (ITEMS, ITEMS), 0)
    columns = lax.broadcasted_iota(jnp.int32, (ITEMS, ITEMS), 1)
    codes = jnp.broadcast_to(bins[...] * 4 + groups[...], (ITEMS, ITEMS))
    code = jnp.sum(jnp.where(rows == columns, codes, 0), axis=1, keepdims=True)
    entry = lax.broadcasted_iota(jnp.int32, (ITEMS, 128), 0)
    place = lax.broadcasted_iota(jnp.int32, (ITEMS, 128), 1)
    match = (jnp.broadcast_to(code, (ITEMS, 128)) == place) & (entry < count[0, 0])
    low = jnp.min(jnp.where(match, entry, EMPTY), axis=0, keepdims=True)
    high = jnp.max(jnp.where(match, entry, -1), axis=0, keepdims=True)
    table[0:1, :] = low
    table[1:2, :] = jnp.where(high > low, high, EMPTY)

    for copy in inputs[3:]:
        copy.wait()
    normal = [norms[c : c + 1, :] for c in range(3)]
    speed = veloc[0] * normal[0] + veloc[1] * normal[1] + veloc[2] * normal[2]
    faces[3] = dens[...] * speed
    for c in range(3):
        faces[c] = press[...] * normal[c] + dens[...] * veloc[c] * speed
    for c in range(3):
        terms[c] = 0.5 * (faces[c, 2:34, :] - faces[c, 0:32, :])
        terms[3 + c] = faces[c, 1:33, :]
    thick[...] = (0.5 * (faces[3, 2:34, :] - faces[3, 0:32, :])).astype(jnp.bfloat16)

    def blocks(half, chunk):
        matrix_copy(half, chunk).wait()
        for item in range(chunk * CHUNK, (chunk + 1) * CHUNK):
            if half == 0:
                d0, d1, d2 = head[0, 0, item], head[1, 0, item], head[2, 0, item]
                rate = d0 * terms[0] + d1 * terms[1] + d2 * terms[2]
                radial = d0 * terms[3] + d1 * terms[4] + d2 * terms[5]
                source = jnp.concatenate(
                    [thick[...], rate.astype(jnp.bfloat16), radial.astype(jnp.bfloat16)], axis=1
                )
                sources[item] = source
            else:
                source = sources[item]
            own[half][item] = jnp.dot(
                source, matrices[half, item], preferred_element_type=jnp.float32
            )

    def pass_on(half, chunk):
        part = pl.ds(chunk * CHUNK, CHUNK)
        return send(own[half].at[part], other[half].at[part], partner)

    def assemble(half):
        for rx in range(4):
            for ry in range(4):
                for rz in range(4):
                    gx = lax.rem(here[0] + rx, 4)
                    gy = lax.rem(here[1] + ry, 4)
                    gz = lax.rem(here[2] + rz, 4)
                    where = ((gx * 4 + gy) * 2 + core) * 4 + gz
                    total = (
                        own[half][look[0, where]]
                        + own[half][look[1, where]]
                        + other[half][look_there[0, where]]
                        + other[half][look_there[1, where]]
                    )
                    for row in range(4):
                        tile = half * 4 + row
                        r = (rx, ry, rz)
                        a, b, c = (r[axis] for axis in PATHS[tile])
                        acc[tile, a, b, c] = total[row * 8 : row * 8 + 8, :]

    waits = {}

    def begin(tile):
        axis = PATHS[tile][0]
        ahead, behind = at(axis, 1), at(axis, 3)
        into = first_in
        part = acc.at[tile]
        lo, hi = pl.ds(0, 2), pl.ds(2, 2)
        waits[tile, 1] = [
            send(part.at[2, lo], into.at[tile, 0], ahead),
            send(part.at[2, hi], into.at[tile, 1], behind),
        ]
        waits[tile, 2] = [
            send(part.at[1, hi], into.at[tile, 2], ahead),
            send(part.at[3, lo], into.at[tile, 3], behind),
        ]

    def go_on(tile, step):
        for copy in waits[tile, step]:
            copy.wait_recv()
        if step == 1:
            axis = PATHS[tile][0]
            acc[tile, 1, 0:2] += first_in[tile, 0]
            acc[tile, 3, 2:4] += first_in[tile, 1]
            waits[tile, 2] += [
                send(acc.at[tile, 1, pl.ds(0, 2)], first_in.at[tile, 4], at(axis, 1)),
                send(acc.at[tile, 3, pl.ds(2, 2)], first_in.at[tile, 5], at(axis, 3)),
            ]
        elif step == 2:
            axis = PATHS[tile][1]
            acc[tile, 0, 0:2] += first_in[tile, 3] + first_in[tile, 4]
            acc[tile, 0, 2:4] += first_in[tile, 2] + first_in[tile, 5]
            waits[tile, 3] = [
                send(acc.at[tile, 0, r], second_in.at[tile, r - 1], at(axis, r)) for r in (2, 1, 3)
            ]
        elif step == 3:
            axis = PATHS[tile][2]
            acc[tile, 0, 0] += second_in[tile, 0] + second_in[tile, 1] + second_in[tile, 2]
            waits[tile, 4] = [
                send(acc.at[tile, 0, 0, r], third_in.at[tile, r - 1], at(axis, r)) for r in (2, 1, 3)
            ]
        else:
            half, row = divmod(tile, 4)
            out_ref[row * 8 : row * 8 + 8, half * HALF : (half + 1) * HALF] = (
                acc[tile, 0, 0, 0] + third_in[tile, 0] + third_in[tile, 1] + third_in[tile, 2]
            )

    blocks(0, 0)
    pl.semaphore_wait(barrier, len(greeted))
    look_copy = pltpu.make_async_copy(table, look, look_sem.at[0])
    look_copy.start()
    table_copy = send(table, table_there, partner)
    passed = [pass_on(0, 0)]
    for chunk in range(1, CHUNKS):
        blocks(0, chunk)
        passed.append(pass_on(0, chunk))
    passed_second = []
    for chunk in range(0, 4):
        blocks(1, chunk)
        passed_second.append(pass_on(1, chunk))
    table_copy.wait_recv()
    look_there_copy = pltpu.make_async_copy(table_there, look_there, look_sem.at[1])
    look_there_copy.start()
    look_copy.wait()
    look_there_copy.wait()
    for copy in passed:
        copy.wait_recv()
    assemble(0)
    for tile in range(4):
        begin(tile)
    for chunk in range(4, CHUNKS):
        blocks(1, chunk)
        passed_second.append(pass_on(1, chunk))
    for copy in passed_second:
        copy.wait_recv()
    assemble(1)
    for tile in range(4, 8):
        begin(tile)
    for tile, step in ORDER:
        go_on(tile, step)
    for copy in sent:
        copy.wait_send()


def local(
    density, velocity, pressure, normal, direction, weights, bin_index, group_index, item_count
):
    in_hbm = pl.BlockSpec(memory_space=pltpu.HBM)
    f32, bf16, i32 = jnp.float32, jnp.bfloat16, jnp.int32
    copies = 1 + 2 * CHUNKS + 8 * 12
    return pl.pallas_call(
        kernel,
        out_shape=jax.ShapeDtypeStruct((STEPS, FACES), f32),
        in_specs=[in_hbm] * 9,
        out_specs=pl.BlockSpec(memory_space=pltpu.VMEM),
        scratch_shapes=[
            pltpu.VMEM((STEPS + 2, FACES), f32),
            pltpu.VMEM((3, STEPS + 2, FACES), f32),
            pltpu.VMEM((STEPS + 2, FACES), f32),
            pltpu.VMEM((3, FACES), f32),
            pltpu.SMEM((3, 1, ITEMS), f32),
            pltpu.VMEM((1, ITEMS), i32),
            pltpu.VMEM((1, ITEMS), i32),
            pltpu.SMEM((1, 1), i32),
            pltpu.VMEM((4, STEPS + 2, FACES), f32),
            pltpu.VMEM((6, STEPS, FACES), f32),
            pltpu.VMEM((STEPS, FACES), bf16),
            pltpu.VMEM((ITEMS, STEPS, 3 * FACES), bf16),
            pltpu.VMEM((2, ITEMS, 3 * FACES, HALF), bf16),
            pltpu.VMEM((ITEMS + 1, STEPS, HALF), f32),
            pltpu.VMEM((ITEMS + 1, STEPS, HALF), f32),
            pltpu.VMEM((ITEMS + 1, STEPS, HALF), f32),
            pltpu.VMEM((ITEMS + 1, STEPS, HALF), f32),
            pltpu.VMEM((2, 128), i32),
            pltpu.VMEM((2, 128), i32),
            pltpu.SMEM((2, 128), i32),
            pltpu.SMEM((2, 128), i32),
            pltpu.VMEM((8, 4, 4, 4, 8, 128), f32),
            pltpu.VMEM((8, 6, 2, 4, 8, 128), f32),
            pltpu.VMEM((8, 3, 4, 8, 128), f32),
            pltpu.VMEM((8, 3, 8, 128), f32),
            pltpu.SemaphoreType.DMA((8,)),
            pltpu.SemaphoreType.DMA((2 * CHUNKS,)),
            pltpu.SemaphoreType.DMA((2,)),
            pltpu.SemaphoreType.DMA((copies,)),
            pltpu.SemaphoreType.DMA((copies,)),
        ],
        compiler_params=pltpu.CompilerParams(
            collective_id=0, has_side_effects=True, vmem_limit_bytes=56 * 1024 * 1024
        ),
    )(
        density,
        velocity,
        pressure,
        normal,
        direction.transpose(2, 0, 1),
        weights.reshape(weights.shape[1:]),
        bin_index,
        group_index,
        item_count.reshape(1, 1),
    )


def solution(mesh):
    placed = (
        P(None, ("obs", "face")),
        P(None, None, ("obs", "face")),
        P(None, ("obs", "face")),
        P(None, ("obs", "face")),
        P(("obs", "face"), None, None),
        P(("obs", "face"), None, None, None),
        P(("obs", "face"), None),
        P(("obs", "face"), None),
        P(("obs", "face")),
    )
    return jax.shard_map(
        local, mesh=mesh, in_specs=placed, out_specs=P("face", "obs"), check_vma=False
    )
```

time: 289 us -> 38.8 us (0.13)
  the two profiles are of different devices: /device:TPU:1 before, /device:TPU:0 now
where the time goes in v1:
time: 38.8 us; the launch traced here: 38.6 us
  Pallas kernels  36.6 us (94%)
  local copies, waits for them, and re-layouts  1.38 us (4%)
  between operations  0.66 us (2%)
    pallas_call x1, Pallas kernels, local(): pl.pallas_call(kernel, out_shape=jax.ShapeDtypeStruct((STEPS, FACES), f32...  36.6 us
    unnamed x1, local copies, waits for them, and re-layouts  1.38 us

profile of v1, /device:TPU:0, one launch (start us, length us, event | category | flops | bytes accessed | tf_op | source)
XLA Modules:
  0.0 38.6 jit_solution(17308188175157385730)
XLA Ops:
  0.7 36.6 %shard_map.91 = f32[32,256]{1,0:T(8,128)} custom-call(f32[34,256]{1,0:T(8,128)} %dens_hbm.1, f32[3,34,256]{2,1,0:T(8,128)} %veloc_hbm.1, f32[34,256]{1,0:T(8,128)} %press_hbm.1, f32[3,256]{1,0:T(4,128)} %norm_hbm.1, f32[3,1,32]{2,1,0:T(1,128)} %bitcast.5, bf16[32,768,256]{2,1,0:T(8,128)(2,1)} %bitcast.4, s32[1,32]{1,0:T(1,128)} %bin_hbm.1, ...), custom_call_target="tpu_custom_call" | custom-call | tf_op jit(solution)/shard_map/pallas_call | solution.py:273
  37.2 1.4 %copy.12 = f32[32,256]{1,0:T(8,128)} copy(f32[32,256]{1,0:T(8,128)} %shard_map.91) | data formatting | bytes 65536
